TPU v7x, 16 devices: a whole 2x2x2 slice. The times are simulated.
16 devices in a mesh: dp: 4 (over z, y), tp: 4 (over x, core).
Axes of the slice: x: 2, y: 2, z: 2, core: 2. Of those that a mesh axis runs over, the one named last changes fastest.
Arguments:
- hidden_in: bfloat16 [4, 256, 6144], P('dp'), parts along dimension 0
- lengths: int32 [4], P('dp'), parts along dimension 0
- positions: int32 [4, 256], P('dp'), parts along dimension 0
- ln_gain: float32 [2, 2, 6144], replicated
- ln_bias: float32 [2, 2, 6144], replicated
- w_query: bfloat16 [2, 6144, 48, 128], P(None, None, 'tp')
- w_key: bfloat16 [2, 6144, 8, 128], replicated
- w_value: bfloat16 [2, 6144, 8, 128], replicated
- w_out: bfloat16 [2, 48, 128, 6144], P(None, 'tp')
- w_up: bfloat16 [2, 6144, 24576], P(None, None, 'tp')
- w_down: bfloat16 [2, 24576, 6144], P(None, 'tp')
Outputs:
- output 1: bfloat16 [4, 256, 6144], P('dp'), parts along dimension 0
- output 2: bfloat16 [2, 4, 256, 8, 128], P(None, 'dp', None, 'tp'), parts along dimension 1
- output 3: bfloat16 [2, 4, 256, 8, 128], P(None, 'dp', None, 'tp'), parts along dimension 1
There are 4 independent parts. A program takes and returns all parts, laid end to end along the dimension named above; an argument that names none is the same for every part.
All inputs are finite; a program needn't handle non-finite values.
Results may differ from a plain program's by a relative error of at most 0.02.
Values are sent between devices in bfloat16 or wider.
A program may use at most 1.75 GiB of HBM per device.

v0:
```python
import jax
import jax.numpy as jnp
from jax import lax
from jax.sharding import PartitionSpec as P

ROPE_BASE = 10000.0
NORM_EPS = 1e-5


def layer_norm(hidden, gain, bias):
    values = hidden.astype(jnp.float32)
    average = jnp.mean(values, axis=-1, keepdims=True)
    centred = values - average
    variance = jnp.mean(centred * centred, axis=-1, keepdims=True)
    normed = centred * lax.rsqrt(variance + NORM_EPS) * (1.0 + gain) + bias
    return normed.astype(jnp.bfloat16)


def rotary_embed(values, positions):
    half_width = values.shape[-1] // 4
    rot_width = 2 * half_width
    frequencies = ROPE_BASE ** (-2.0 * jnp.arange(half_width, dtype=jnp.float32) / rot_width)
    angles = positions.astype(jnp.float32)[..., None] * frequencies
    cosine = jnp.cos(angles)[..., None, :]
    sine = jnp.sin(angles)[..., None, :]
    first = values[..., :half_width]
    second = values[..., half_width:rot_width]
    return jnp.concatenate([first * cosine - second * sine, second * cosine + first * sine, values[..., rot_width:]], axis=-1)


def solution(mesh):
    tp_size = mesh.shape["tp"]

    def device_body(hidden_in, lengths, positions, ln_gain, ln_bias, w_query, w_key, w_value, w_out, w_up, w_down):
        batch, seq_len = hidden_in.shape[0], hidden_in.shape[1]
        kv_heads = w_key.shape[2]
        head_dim = w_key.shape[3]
        head_local = w_query.shape[2]
        kv_local = max(kv_heads // tp_size, 1)
        share = max(tp_size // kv_heads, 1)
        group = head_local // kv_local
        scale = head_dim ** -0.5
        tp_index = lax.axis_index("tp")
        kv_start = (tp_index // share) * kv_local
        query_pos = jnp.arange(seq_len)[:, None]
        key_pos = jnp.arange(seq_len)[None, :]
        allowed = ((key_pos <= query_pos)[None] & (key_pos[None] < lengths[:, None, None]))[:, None, None]
        valid = (jnp.arange(seq_len)[None, :] < lengths[:, None])[:, :, None, None]
        hidden = hidden_in
        key_layers = []
        value_layers = []
        for layer in range(w_query.shape[0]):
            k_weight = lax.dynamic_slice_in_dim(w_key[layer], kv_start, kv_local, axis=1)
            v_weight = lax.dynamic_slice_in_dim(w_value[layer], kv_start, kv_local, axis=1)
            normed = layer_norm(hidden, ln_gain[layer, 0], ln_bias[layer, 0])
            query_lin = jnp.einsum("bsd,dhe->bshe", normed, w_query[layer], preferred_element_type=jnp.float32)
            key_lin = jnp.einsum("bsd,dhe->bshe", normed, k_weight, preferred_element_type=jnp.float32)
            value_lin = jnp.einsum("bsd,dhe->bshe", normed, v_weight, preferred_element_type=jnp.float32)
            query = rotary_embed(query_lin, positions).astype(jnp.bfloat16).reshape(batch, seq_len, kv_local, group, head_dim)
            keys = rotary_embed(key_lin, positions).astype(jnp.bfloat16)
            values = value_lin.astype(jnp.bfloat16)
            scores = jnp.einsum("bqkgd,bskd->bkgqs", query, keys, preferred_element_type=jnp.float32) * scale
            attn_weights = jax.nn.softmax(jnp.where(allowed, scores, -1e30), axis=-1).astype(jnp.bfloat16)
            mixed = jnp.einsum("bkgqs,bskd->bqkgd", attn_weights, values, preferred_element_type=jnp.float32).astype(jnp.bfloat16)
            mixed = mixed.reshape(batch, seq_len, head_local, head_dim)
            attn_part = jnp.einsum("bshe,hed->bsd", mixed, w_out[layer], preferred_element_type=jnp.float32).astype(jnp.bfloat16)
            attn_sum = lax.psum(attn_part, "tp")
            residual = (hidden.astype(jnp.float32) + attn_sum.astype(jnp.float32)).astype(jnp.bfloat16)
            normed_mlp = layer_norm(residual, ln_gain[layer, 1], ln_bias[layer, 1])
            up_lin = jnp.einsum("bsd,df->bsf", normed_mlp, w_up[layer], preferred_element_type=jnp.float32)
            activated = jnp.maximum(up_lin, 0.0)
            activated = (activated * activated).astype(jnp.bfloat16)
            mlp_part = jnp.einsum("bsf,fd->bsd", activated, w_down[layer], preferred_element_type=jnp.float32).astype(jnp.bfloat16)
            mlp_sum = lax.psum(mlp_part, "tp")
            hidden = (residual.astype(jnp.float32) + mlp_sum.astype(jnp.float32)).astype(jnp.bfloat16)
            key_layers.append(jnp.where(valid, keys, 0.0).astype(jnp.bfloat16))
            value_layers.append(jnp.where(valid, values, 0.0).astype(jnp.bfloat16))
        return hidden, jnp.stack(key_layers), jnp.stack(value_layers)

    specs_in = (P("dp", None, None), P("dp"), P("dp", None), P(), P(), P(None, None, "tp", None), P(), P(), P(None, "tp", None, None), P(None, None, "tp"), P(None, "tp", None))
    cache_spec = P(None, "dp", None, "tp", None)
    return jax.shard_map(device_body, mesh=mesh, in_specs=specs_in, out_specs=(P("dp", None, None), cache_spec, cache_spec), check_vma=False)
```

profile of v0, /device:TPU:0, one launch (start us, length us, event | category | flops | bytes accessed | tf_op | source)
XLA Modules:
  0.0 603.3 jit_solution(17577803232067570015)
XLA Ops:
  7.2 24.7 %fusion.212 = (bf16[1,6144,12,128]{3,1,2,0:T(8,128)(2,1)}, bf16[1,6144,12,128]{3,1,2,0:T(8,128)(2,1)}) fusion(bf16[2,6144,12,128]{3,1,2,0:T(8,128)(2,1)} %param.16), kind=kLoop, calls=%fused_computation.198 | loop fusion | bytes 75497472 | tf_op jit(solution)/shard_map/slice | solution.py:56
  32.0 23.5 %copy.52 = bf16[1,6144,12,128]{1,3,2,0:T(8,128)(2,1)} copy(bf16[1,6144,12,128]{3,1,2,0:T(8,128)(2,1)} %get-tuple-element.12) | data formatting | bytes 37748736
  58.4 9.3 %fusion.120 = f32[256,1536]{0,1:S(1)} fusion(bf16[6144,1536]{0,1:T(8,128)(2,1)} %bitcast.286, bf16[1,256,6144]{2,1,0:T(8,128)(2,1)S(1)} %copy-done, f32[6144]{0:T(1024)S(1)} %bitcast.321, f32[6144]{0:T(1024)S(1)} %bitcast.324, f32[256]{0:T(256)S(1)} %add_rsqrt_fusion.3, f32[256]{0:T(256)S(1)} %broadcast_multiply_fusion.3), kind=kOutput, calls=%fused_computation.90 | convolution fusion | flops 4841275392 | bytes 23644160
  69.7 17.0 %fusion.214 = (bf16[1,6144,8,128]{3,2,1,0:T(8,128)(2,1)}, bf16[1,6144,8,128]{3,2,1,0:T(8,128)(2,1)}) fusion(bf16[2,6144,8,128]{3,2,1,0:T(8,128)(2,1)} %param.17), kind=kLoop, calls=%fused_computation.200 | loop fusion | bytes 50331648 | tf_op jit(solution)/shard_map/slice | solution.py:53
  86.6 13.8 %constant_dynamic-slice_fusion = (bf16[1,6144,2,128]{3,2,1,0:T(2,128)(2,1)}, bf16[1,6144,2,128]{3,2,1,0:T(2,128)(2,1)}) fusion(bf16[1,6144,8,128]{3,2,1,0:T(8,128)(2,1)} %get-tuple-element.16, s32[]{:T(128)S(6)} %select_n.49, bf16[1,6144,8,128]{3,2,1,0:T(8,128)(2,1)} %get-tuple-element.17), kind=kLoop, calls=%fused_computation.180 | loop fusion | bytes 12582916 | tf_op jit(solution)/shard_map/dynamic_slice | solution.py:53
  100.5 8.7 %copy.15 = bf16[1,6144,2,128]{1,3,2,0:T(8,128)(2,1)} copy(bf16[1,6144,2,128]{3,2,1,0:T(2,128)(2,1)} %get-tuple-element.49) | data formatting | bytes 6291456 | tf_op jit(solution)/shard_map/dynamic_slice | solution.py:53
  109.2 3.5 fusion.118
  115.6 2.2 copy.19
  117.8 2.1 copy.18
  121.1 13.2 %fusion.213 = (bf16[1,6144,8,128]{3,2,1,0:T(8,128)(2,1)}, bf16[1,6144,8,128]{3,2,1,0:T(8,128)(2,1)S(1)}) fusion(bf16[2,6144,8,128]{3,2,1,0:T(8,128)(2,1)} %param.18), kind=kLoop, calls=%fused_computation.199 | loop fusion | bytes 50331648 | tf_op jit(solution)/shard_map/slice | solution.py:54
  134.3 3.8 constant_dynamic-slice_fusion.3
  143.0 10.2 %fusion.66 = bf16[1,256,6144]{2,1,0:T(8,128)(2,1)} fusion(bf16[256,12,128]{0,2,1:T(8,128)(2,1)S(1)} %bitcast.329, bf16[2,12,128,6144]{3,2,1,0:T(8,128)(2,1)} %param.19), kind=kOutput, calls=%fused_computation.50 | convolution fusion | flops 4833411072 | bytes 22806528 | tf_op jit(solution)/shard_map/bshe,hed->bsd/dot_general | solution.py:66
  153.3 67.4 %all-reduce.5.cloned.1.call-done = bf16[1,256,6144]{2,1,0:T(8,128)(2,1)} async-done(((bf16[1,256,6144]{2,1,0:T(8,128)(2,1)}), bf16[1,256,6144]{2,1,0:T(8,128)(2,1)}) %all-reduce.5.cloned.1.call-update) | async-done | bytes 3145744 | tf_op jit(solution)/shard_map/psum | solution.py:67
  220.8 3.1 convert_reduce_fusion.2
  226.6 32.0 %fusion.39.clone.7 = bf16[256,6144]{1,0:T(8,128)(2,1)} fusion(bf16[2,6144,6144]{2,1,0:T(8,128)(2,1)} %param.20, bf16[1,256,6144]{2,1,0:T(8,128)(2,1)} %copy-done.1, f32[6144]{0:T(1024)S(1)} %bitcast.319, f32[6144]{0:T(1024)S(1)} %bitcast.320, f32[256]{0:T(256)S(1)} %add_rsqrt_fusion.2, f32[256]{0:T(256)S(1)} %broadcast_multiply_fusion.2), kind=kOutput, calls=%fused_computation.37.clone.clone.clone.clone.clone.2 | convolution fusion | flops 19341508608 | bytes 81840128 | tf_op jit(solution)/shard_map/bsd,df->bsf/dot_general | solution.py:70
  258.6 30.9 %fusion.77 = bf16[1,256,6144]{2,1,0:T(8,128)(2,1)} fusion(bf16[2,6144,6144]{2,1,0:T(8,128)(2,1)} %param.21, bf16[256,6144]{1,0:T(8,128)(2,1)} %fusion.39.clone.7), kind=kOutput, calls=%fused_computation.53 | convolution fusion | flops 19328925696 | bytes 81788928 | tf_op jit(solution)/shard_map/bsf,fd->bsd/dot_general | solution.py:73
  289.6 23.5 %copy.53 = bf16[1,6144,12,128]{1,3,2,0:T(8,128)(2,1)} copy(bf16[1,6144,12,128]{3,1,2,0:T(8,128)(2,1)} %get-tuple-element.13) | data formatting | bytes 37748736
  313.1 5.5 copy.25
  318.6 8.7 %constant_dynamic-slice_fusion.1 = bf16[1,6144,2,128]{3,2,1,0:T(2,128)(2,1)} fusion(bf16[1,6144,8,128]{3,2,1,0:T(8,128)(2,1)} %get-tuple-element.14, s32[]{:T(128)S(6)} %select_n.49), kind=kLoop, calls=%fused_computation.181 | loop fusion | bytes 6291460 | tf_op jit(solution)/shard_map/dynamic_slice | solution.py:54
  327.3 27.0 %all-reduce.7.cloned.1.call-done = bf16[1,256,6144]{2,1,0:T(8,128)(2,1)} async-done(((bf16[1,256,6144]{2,1,0:T(8,128)(2,1)}), bf16[1,256,6144]{2,1,0:T(8,128)(2,1)}) %all-reduce.7.cloned.1.call-update) | async-done | bytes 3145744 | tf_op jit(solution)/shard_map/psum | solution.py:74
  354.3 4.1 convert_reduce_fusion.1
  359.5 9.6 %fusion.113 = f32[256,1536]{0,1:S(1)} fusion(bf16[6144,1536]{0,1:T(8,128)(2,1)} %bitcast.285, bf16[1,256,6144]{2,1,0:T(8,128)(2,1)S(1)} %get-tuple-element.9, f32[6144]{0:T(1024)S(1)} %bitcast.314, f32[6144]{0:T(1024)S(1)} %bitcast.317, f32[256]{0:T(256)S(1)} %add_rsqrt_fusion.1, f32[256]{0:T(256)S(1)} %broadcast_multiply_fusion.1), kind=kOutput, calls=%fused_computation.83 | convolution fusion | flops 4841275392 | bytes 23644160
  374.0 2.1 copy.28
  376.1 2.1 copy.27
  378.2 3.6 fusion.163
  385.1 10.2 %fusion.69 = bf16[1,256,6144]{2,1,0:T(8,128)(2,1)} fusion(bf16[256,12,128]{0,2,1:T(8,128)(2,1)S(1)} %bitcast.328, bf16[2,12,128,6144]{3,2,1,0:T(8,128)(2,1)} %param.19), kind=kOutput, calls=%fused_computation.51 | convolution fusion | flops 4833411072 | bytes 22806528 | tf_op jit(solution)/shard_map/bshe,hed->bsd/dot_general | solution.py:66
  395.4 64.7 %all-reduce.9.cloned.1.call-done = bf16[1,256,6144]{2,1,0:T(8,128)(2,1)} async-done(((bf16[1,256,6144]{2,1,0:T(8,128)(2,1)}), bf16[1,256,6144]{2,1,0:T(8,128)(2,1)}) %all-reduce.9.cloned.1.call-update) | async-done | bytes 3145744 | tf_op jit(solution)/shard_map/psum | solution.py:67
  460.1 3.1 convert_reduce_fusion
  465.9 30.9 %fusion.36.clone.7 = bf16[256,6144]{1,0:T(8,128)(2,1)S(1)} fusion(bf16[2,6144,6144]{2,1,0:T(8,128)(2,1)} %param.20, bf16[1,256,6144]{2,1,0:T(8,128)(2,1)} %copy-done.2, f32[6144]{0:T(1024)S(1)} %bitcast.311, f32[6144]{0:T(1024)S(1)} %bitcast.312, f32[256]{0:T(256)S(1)} %add_rsqrt_fusion, f32[256]{0:T(256)S(1)} %broadcast_multiply_fusion), kind=kOutput, calls=%fused_computation.36.clone.clone.clone.clone.clone.2 | convolution fusion | flops 19341508608 | bytes 81840128 | tf_op jit(solution)/shard_map/bsd,df->bsf/dot_general | solution.py:70
  496.9 30.0 %fusion.72 = bf16[1,256,6144]{2,1,0:T(8,128)(2,1)} fusion(bf16[2,6144,6144]{2,1,0:T(8,128)(2,1)} %param.21, bf16[256,6144]{1,0:T(8,128)(2,1)S(1)} %fusion.36.clone.7), kind=kOutput, calls=%fused_computation.52 | convolution fusion | flops 19328925696 | bytes 81788928 | tf_op jit(solution)/shard_map/bsf,fd->bsd/dot_general | solution.py:73
  529.9 61.8 %all-reduce.11.cloned.1.call-done = bf16[1,256,6144]{2,1,0:T(8,128)(2,1)} async-done(((bf16[1,256,6144]{2,1,0:T(8,128)(2,1)}), bf16[1,256,6144]{2,1,0:T(8,128)(2,1)}) %all-reduce.11.cloned.1.call-update) | async-done | bytes 3145744 | tf_op jit(solution)/shard_map/psum | solution.py:74
  591.7 4.7 fusion.101
  (150 shorter events, 30.5 us)
Async XLA Ops:
  7.2 213.6 %all-reduce.5.cloned.1.call-start = ((), (), s32[]{:S(2)}) async-start(), calls=%async_computation | async-start | bytes 6291456 | tf_op jit(solution)/shard_map/psum | solution.py:67
  31.9 23.6 %copy-start.32 = (f32[2,2,6144]{2,1,0:T(2,128)S(1)}, f32[2,2,6144]{2,1,0:T(2,128)}, u32[]{:S(2)}) copy-start(f32[2,2,6144]{2,1,0:T(2,128)} %param.15) | copy-start | bytes 294916
  31.9 24.2 %copy-start.33 = (f32[2,2,6144]{2,1,0:T(2,128)S(1)}, f32[2,2,6144]{2,1,0:T(2,128)}, u32[]{:S(2)}) copy-start(f32[2,2,6144]{2,1,0:T(2,128)} %param.14) | copy-start | bytes 294916
  32.0 24.9 %copy-start = (bf16[1,256,6144]{2,1,0:T(8,128)(2,1)S(1)}, bf16[1,256,6144]{2,1,0:T(8,128)(2,1)}, u32[]{:S(2)}) copy-start(bf16[1,256,6144]{2,1,0:T(8,128)(2,1)} %param.11) | copy-start | bytes 9437188
  56.2 53.0 %copy-start.42 = (f32[1,1,6144]{2,1,0:T(1,128)}, f32[1,1,6144]{2,1,0:T(1,128)S(1)}, u32[]{:S(2)}) copy-start(f32[1,1,6144]{2,1,0:T(1,128)S(1)} %get-tuple-element.36) | copy-start | bytes 73732
  56.9 52.3 %copy-start.44 = (f32[1,1,6144]{2,1,0:T(1,128)}, f32[1,1,6144]{2,1,0:T(1,128)S(1)}, u32[]{:S(2)}) copy-start(f32[1,1,6144]{2,1,0:T(1,128)S(1)} %get-tuple-element.32) | copy-start | bytes 73732
  58.4 11.3 %copy-start.48 = (s32[1,256]{1,0:T(1,128)S(1)}, s32[1,256]{1,0:T(1,128)}, u32[]{:S(2)}) copy-start(s32[1,256]{1,0:T(1,128)} %param.13) | copy-start | bytes 3076
  114.4 25.5 %copy-start.20 = (bf16[1,256,2,32]{1,3,2,0:T(8,128)(2,1)}, bf16[1,256,2,32]{1,3,2,0:T(8,128)(2,1)S(1)}, u32[]{:S(2)}) copy-start(bf16[1,256,2,32]{1,3,2,0:T(8,128)(2,1)S(1)} %get-tuple-element.24) | copy-start | bytes 98308
  114.4 25.5 %copy-start.22 = (bf16[1,256,2,32]{1,3,2,0:T(8,128)(2,1)}, bf16[1,256,2,32]{1,3,2,0:T(8,128)(2,1)S(1)}, u32[]{:S(2)}) copy-start(bf16[1,256,2,32]{1,3,2,0:T(8,128)(2,1)S(1)} %get-tuple-element.25) | copy-start | bytes 98308
  115.6 26.3 %copy-start.12 = (pred[256,256]{0,1:T(8,128)(4,1)}, pred[256,256]{0,1:T(8,128)(4,1)S(1)}, u32[]{:S(2)}) copy-start(pred[256,256]{0,1:T(8,128)(4,1)S(1)} %fusion.180) | copy-start | bytes 196612
  153.3 73.3 %copy-start.40 = (f32[1,1,6144]{2,1,0:T(1,128)S(1)}, f32[1,1,6144]{2,1,0:T(1,128)}, u32[]{:S(2)}) copy-start(f32[1,1,6144]{2,1,0:T(1,128)} %get-tuple-element.35) | copy-start | bytes 73732
  153.3 73.3 %copy-start.41 = (f32[1,1,6144]{2,1,0:T(1,128)S(1)}, f32[1,1,6144]{2,1,0:T(1,128)}, u32[]{:S(2)}) copy-start(f32[1,1,6144]{2,1,0:T(1,128)} %get-tuple-element.31) | copy-start | bytes 73732
  153.3 201.0 %all-reduce.7.cloned.1.call-start = ((), (), s32[]{:S(2)}) async-start(), calls=%async_computation.1 | async-start | bytes 6291456 | tf_op jit(solution)/shard_map/psum | solution.py:74
  289.5 170.6 %all-reduce.9.cloned.1.call-start = ((), (), s32[]{:S(2)}) async-start(), calls=%async_computation.2 | async-start | bytes 6291456 | tf_op jit(solution)/shard_map/psum | solution.py:67
  289.6 23.5 %copy-start.4 = (bf16[1,6144,2,128]{3,2,1,0:T(2,128)(2,1)S(1)}, bf16[1,6144,2,128]{3,2,1,0:T(2,128)(2,1)}, u32[]{:S(2)}) copy-start(bf16[1,6144,2,128]{3,2,1,0:T(2,128)(2,1)} %get-tuple-element.48) | copy-start | bytes 9437188
  327.3 32.1 %copy-start.36 = (f32[1,1,6144]{2,1,0:T(1,128)S(1)}, f32[1,1,6144]{2,1,0:T(1,128)}, u32[]{:S(2)}) copy-start(f32[1,1,6144]{2,1,0:T(1,128)} %get-tuple-element.37) | copy-start | bytes 73732
  327.3 32.1 %copy-start.38 = (f32[1,1,6144]{2,1,0:T(1,128)S(1)}, f32[1,1,6144]{2,1,0:T(1,128)}, u32[]{:S(2)}) copy-start(f32[1,1,6144]{2,1,0:T(1,128)} %get-tuple-element.33) | copy-start | bytes 73732
  359.4 9.7 %copy-start.17 = (f32[256,32]{0,1:T(8,128)S(1)}, f32[256,32]{0,1:T(8,128)}, u32[]{:S(2)}) copy-start(f32[256,32]{0,1:T(8,128)} %copy-done.16) | copy-start | bytes 98308
  359.4 9.7 %copy-start.19 = (f32[256,32]{0,1:T(8,128)S(1)}, f32[256,32]{0,1:T(8,128)}, u32[]{:S(2)}) copy-start(f32[256,32]{0,1:T(8,128)} %copy-done.18) | copy-start | bytes 98308
  359.4 10.6 %copy-start.5 = (bf16[1,6144,2,128]{1,3,2,0:T(8,128)(2,1)S(1)}, bf16[1,6144,2,128]{1,3,2,0:T(8,128)(2,1)}, u32[]{:S(2)}) copy-start(bf16[1,6144,2,128]{1,3,2,0:T(8,128)(2,1)} %copy.25) | copy-start | bytes 9437188
  359.4 10.6 %copy-start.37 = (f32[1,1,6144]{2,1,0:T(1,128)S(1)}, f32[1,1,6144]{2,1,0:T(1,128)}, u32[]{:S(2)}) copy-start(f32[1,1,6144]{2,1,0:T(1,128)} %get-tuple-element.37) | copy-start | bytes 73732
  359.5 10.6 %copy-start.39 = (f32[1,1,6144]{2,1,0:T(1,128)S(1)}, f32[1,1,6144]{2,1,0:T(1,128)}, u32[]{:S(2)}) copy-start(f32[1,1,6144]{2,1,0:T(1,128)} %get-tuple-element.33) | copy-start | bytes 73732
  395.3 70.6 %copy-start.34 = (f32[1,1,6144]{2,1,0:T(1,128)S(1)}, f32[1,1,6144]{2,1,0:T(1,128)}, u32[]{:S(2)}) copy-start(f32[1,1,6144]{2,1,0:T(1,128)} %get-tuple-element.34) | copy-start | bytes 73732
  395.3 70.6 %copy-start.35 = (f32[1,1,6144]{2,1,0:T(1,128)S(1)}, f32[1,1,6144]{2,1,0:T(1,128)}, u32[]{:S(2)}) copy-start(f32[1,1,6144]{2,1,0:T(1,128)} %get-tuple-element.30) | copy-start | bytes 73732
  395.3 196.3 %all-reduce.11.cloned.1.call-start = ((), (), s32[]{:S(2)}) async-start(), calls=%async_computation.3 | async-start | bytes 6291456 | tf_op jit(solution)/shard_map/psum | solution.py:74
  496.8 30.1 %copy-start.21 = (bf16[1,256,2,32]{1,3,2,0:T(8,128)(2,1)S(1)}, bf16[1,256,2,32]{1,3,2,0:T(8,128)(2,1)}, u32[]{:S(2)}) copy-start(bf16[1,256,2,32]{1,3,2,0:T(8,128)(2,1)} %copy-done.20) | copy-start | bytes 98308
  496.8 30.1 %copy-start.23 = (bf16[1,256,2,32]{1,3,2,0:T(8,128)(2,1)S(1)}, bf16[1,256,2,32]{1,3,2,0:T(8,128)(2,1)}, u32[]{:S(2)}) copy-start(bf16[1,256,2,32]{1,3,2,0:T(8,128)(2,1)} %copy-done.22) | copy-start | bytes 98308
  496.8 30.1 %copy-start.27 = (bf16[1,1,256,2,64]{2,4,3,1,0:T(8,128)(2,1)S(1)}, bf16[1,1,256,2,64]{2,4,3,1,0:T(8,128)(2,1)}, u32[]{:S(2)}) copy-start(bf16[1,1,256,2,64]{2,4,3,1,0:T(8,128)(2,1)} %get-tuple-element.26) | copy-start | bytes 196612
  496.8 30.1 %copy-start.28 = (bf16[1,1,256,2,64]{2,4,3,1,0:T(8,128)(2,1)S(1)}, bf16[1,1,256,2,64]{2,4,3,1,0:T(8,128)(2,1)}, u32[]{:S(2)}) copy-start(bf16[1,1,256,2,64]{2,4,3,1,0:T(8,128)(2,1)} %get-tuple-element.28) | copy-start | bytes 196612
  496.8 30.1 %copy-start.47 = (pred[256]{0:T(512)(128)(4,1)S(1)}, pred[256]{0:T(512)(128)(4,1)}, u32[]{:S(2)}) copy-start(pred[256]{0:T(512)(128)(4,1)} %copy-done.46) | copy-start | bytes 772
  496.8 31.0 %copy-start.30 = (bf16[256,2,128]{2,0,1:T(8,128)(2,1)S(1)}, bf16[256,2,128]{2,0,1:T(8,128)(2,1)}, u32[]{:S(2)}) copy-start(bf16[256,2,128]{2,0,1:T(8,128)(2,1)} %copy-done.29) | copy-start | bytes 393220
  526.8 64.8 %copy-start.3 = (bf16[1,256,6144]{2,1,0:T(8,128)(2,1)S(1)}, bf16[1,256,6144]{2,1,0:T(8,128)(2,1)}, u32[]{:S(2)}) copy-start(bf16[1,256,6144]{2,1,0:T(8,128)(2,1)} %copy-done.2) | copy-start | bytes 9437188
  (21 other events, 57.7 us)
Sparse Core Ops, SparseCore 0:
  153.4 67.3 all-reduce.4
  289.6 64.6 all-reduce.6
  395.4 64.6 all-reduce.8
  527.0 64.6 all-reduce.10
where the time goes:
time: 613 us; the launch traced here: 603 us
  waiting for transfers between devices  221 us (36%)
  matrix products  178 us (29%)
  local copies, waits for them, and re-layouts  163 us (27%)
  other arithmetic  25.3 us (4%)
  between operations  15.7 us (3%)
    psum x2, waiting for transfers between devices, device_body(): attn_sum = lax.psum(attn_part, 'tp')  132 us
    psum x2, waiting for transfers between devices, device_body(): mlp_sum = lax.psum(mlp_part, 'tp')  88.7 us
    dot_general x2, matrix products, device_body(): jnp.einsum('bsd,df->bsf', normed_mlp, w_up[layer], preferred_element_type...  62.9 us
    dot_general x2, matrix products, device_body(): jnp.einsum('bsf,fd->bsd', activated, w_down[layer], preferred_element_typ...  60.9 us
    unnamed x102, local copies, waits for them, and re-layouts  54 us
    dynamic_slice x3, local copies, waits for them, and re-layouts, device_body(): lax.dynamic_slice_in_dim(w_key[layer], kv_start, kv_local, axis=1)  28 us
    slice x1, local copies, waits for them, and re-layouts, device_body(): w_query[layer]  24.7 us
    unnamed x4, matrix products  23.9 us
  transfers between devices with their start and end apart: 4, of which 4 were waited for; matrix products, arithmetic and copies ran while one was open for 7% of the time, Pallas kernels for 0%

commit v1 on v0

v1 whole, which is shorter than its diff:
```python
import functools

import jax
import jax.numpy as jnp
from jax import lax
from jax.experimental import pallas as pl
from jax.experimental.pallas import tpu as pltpu
from jax.sharding import PartitionSpec as P

ROPE_BASE = 10000.0
NORM_EPS = 1e-5
CH = 512
RING = 6
KV_RING = 4
MESH = pl.DeviceIdType.MESH
F32 = jnp.float32
BF16 = jnp.bfloat16


def kernel(cfg, hid, tabs, mask, valid, gain, bias, wq, wk, wv, wo, wu, wd,
           out, kc, vc,
           wbuf, kraw, vraw, wkv, hbuf, acc, abuf, pbuf, rbuf, xrecv, xres,
           wsem, ksem, vsem, iosem,
           d_send, d_recv, x_send, x_recv,
           gx_send, gx_recv, gc_send, gc_recv, gf_send, gf_recv):
    layers, seq, d, heads, scale = cfg
    nch = d // CH
    qw = heads * 128
    nq = qw // CH
    quarter = seq // 4
    half = seq // 2
    kper = nch // nq

    me = lax.axis_index("tp")
    mx = me // 2
    mc = me % 2
    core_peer = {"tp": mx * 2 + (1 - mc)}
    chip_peer = {"tp": (1 - mx) * 2 + mc}
    own_rows = pl.ds(pl.multiple_of(half * mc + quarter * mx, quarter), quarter)
    peer_rows = pl.ds(pl.multiple_of(half * mc + quarter * (1 - mx), quarter), quarter)
    away_rows = pl.ds(pl.multiple_of(half * (1 - mc), half), half)
    own_part = pl.ds(pl.multiple_of(quarter * mx, quarter), quarter)
    peer_part = pl.ds(pl.multiple_of(quarter * (1 - mx), quarter), quarter)

    def cols(j):
        if isinstance(j, int):
            return pl.ds(j * CH, CH)
        return pl.ds(pl.multiple_of(j * CH, CH), CH)

    def fetch_q(l, i, slot):
        rows = kper * CH
        for n in range(nq):
            for hh in range(4):
                pltpu.make_async_copy(
                    wq.at[l, 4 * n + hh, pl.ds(pl.multiple_of(i * rows, rows), rows), :],
                    wbuf.at[slot, pl.ds(n * rows, rows), pl.ds(hh * 128, 128)],
                    wsem.at[slot]).start()

    def fetch_o(l, i, slot):
        for n in range(kper):
            pltpu.make_async_copy(
                wo.at[l, :, cols(i * kper + n)],
                wbuf.at[slot, pl.ds(n * qw, qw), :],
                wsem.at[slot]).start()

    def fetch_u(l, i, slot):
        for n in range(nch):
            pltpu.make_async_copy(
                wu.at[l, cols(i), pl.ds(n * CH, CH)],
                wbuf.at[slot, pl.ds(n * CH, CH), :],
                wsem.at[slot]).start()

    def fetch_d(l, i, slot):
        pltpu.make_async_copy(wd.at[l, :, cols(i)], wbuf.at[slot], wsem.at[slot]).start()

    def weights_ready(slot):
        pltpu.make_async_copy(wd.at[0, :, pl.ds(0, CH)], wbuf.at[slot], wsem.at[slot]).wait()

    def kv_copies(l, kk):
        slot = kk % KV_RING
        rows = cols(kk)
        return (pltpu.make_async_copy(wk.at[l, rows, me], kraw.at[slot], ksem.at[slot]),
                pltpu.make_async_copy(wv.at[l, rows, me], vraw.at[slot], vsem.at[slot]))

    def kv_fetch(l, kk):
        for c in kv_copies(l, kk):
            c.start()

    def remote(src, dst, ssem, rsem, peer):
        return pltpu.make_async_remote_copy(
            src_ref=src, dst_ref=dst, send_sem=ssem, recv_sem=rsem,
            device_id=peer, device_id_type=MESH)

    def d_copy(j):
        return remote(pbuf.at[away_rows, cols(j)], rbuf.at[:, cols(j)],
                      d_send.at[j], d_recv.at[j], core_peer)

    def x_copy(j):
        return remote(pbuf.at[peer_rows, cols(j)], xrecv.at[:, cols(j)],
                      x_send.at[j], x_recv.at[j], chip_peer)

    def rs_mid(j):
        d_copy(j).wait_recv()
        s = pbuf[peer_rows, cols(j)].astype(F32) + rbuf[peer_part, cols(j)].astype(F32)
        pbuf[peer_rows, cols(j)] = s.astype(BF16)
        x_copy(j).start()

    def rs_fin(j):
        x_copy(j).wait_recv()
        s = pbuf[own_rows, cols(j)].astype(F32) + rbuf[own_part, cols(j)].astype(F32)
        s = (s + xrecv[:, cols(j)].astype(F32)).astype(BF16)
        new = (xres[:, cols(j)].astype(F32) + s.astype(F32)).astype(BF16)
        xres[:, cols(j)] = new
        return new

    def gx_copy(j):
        r = hbuf.at[own_rows, cols(j)]
        return remote(r, r, gx_send.at[j], gx_recv.at[j], chip_peer)

    def gc_copy(j):
        r = hbuf.at[own_rows, cols(j)]
        return remote(r, r, gc_send.at[j], gc_recv.at[j], core_peer)

    def gf_copy(j):
        r = hbuf.at[peer_rows, cols(j)]
        return remote(r, r, gf_send.at[j], gf_recv.at[j], core_peer)

    def forward(j):
        gx_copy(j).wait_recv()
        gf_copy(j).start()

    def gathered(j):
        gc_copy(j).wait_recv()
        gf_copy(j).wait_recv()

    def loop(n, body):
        lax.fori_loop(0, n, lambda i, c: (body(i), c)[1], 0)

    def gather_sent():
        def body(j):
            gx_copy(j).wait_send()
            gc_copy(j).wait_send()
            gf_copy(j).wait_send()
        loop(nch, body)

    def norm_rows(src, src_rows, dst_rows, row, after):
        zero = jnp.zeros((quarter, CH), F32)
        total = lax.fori_loop(
            0, nch, lambda j, t: t + src[src_rows, cols(j)].astype(F32), zero)
        mean = jnp.sum(total, axis=-1, keepdims=True) * (1.0 / d)

        def squares(j, t):
            x = src[src_rows, cols(j)].astype(F32) - mean
            return t + x * x

        var = jnp.sum(lax.fori_loop(0, nch, squares, zero), axis=-1, keepdims=True) * (1.0 / d)
        rstd = lax.rsqrt(var + NORM_EPS)

        def write(j):
            x = (src[src_rows, cols(j)].astype(F32) - mean) * rstd
            y = x * (1.0 + gain[pl.ds(row, 1), cols(j)]) + bias[pl.ds(row, 1), cols(j)]
            hbuf[dst_rows, cols(j)] = y.astype(BF16)
            after(j)

        loop(nch, write)

    def norm_and_send(row):
        def after(j):
            gx_copy(j).start()
            gc_copy(j).start()
        norm_rows(xres, pl.ds(0, quarter), own_rows, row, after)

    def clear(width):
        def body(i):
            acc[pl.ds(pl.multiple_of(i * 16, 16), 16), pl.ds(0, width)] = jnp.zeros((16, width), F32)
        loop(seq // 16, body)

    def project(l):
        clear(qw + CH)
        if l > 0:
            forward(0)

        def group(i):
            slot = i
            weights_ready(slot)

            def chunk(kq):
                kk = i * kper + kq
                if l > 0:
                    @pl.when(kk + 1 < nch)
                    def _():
                        forward(kk + 1)
                    gathered(kk)
                for c in kv_copies(l, kk):
                    c.wait()
                ks = kk % KV_RING
                for n in range(2):
                    wkv[:, pl.ds(n * 128, 128)] = kraw[ks, :, n, :]
                    wkv[:, pl.ds((n + 2) * 128, 128)] = vraw[ks, :, n, :]
                hk = hbuf[:, cols(kk)]
                for n in range(nq):
                    w = wbuf[slot, pl.ds(pl.multiple_of(n * kper * CH + kq * CH, CH), CH), :]
                    acc[:, pl.ds(n * CH, CH)] += jnp.dot(hk, w, preferred_element_type=F32)
                acc[:, pl.ds(qw, CH)] += jnp.dot(hk, wkv[...], preferred_element_type=F32)
                if KV_RING:
                    @pl.when(kk + KV_RING < nch)
                    def _():
                        kv_fetch(l, kk + KV_RING)
                    if l + 1 < layers:
                        @pl.when(kk + KV_RING >= nch)
                        def _():
                            kv_fetch(l + 1, kk + KV_RING - nch)

            loop(kper, chunk)
            fetch_u(l, i, slot)

        loop(nq, group)
        if l > 0:
            gather_sent()

    def attention(l):
        cosine, sin_a, sin_b = tabs[0], tabs[1], tabs[2]
        live = valid[...]

        def rope(x):
            return (x * cosine + pltpu.roll(x, 96, 1) * sin_a + pltpu.roll(x, 32, 1) * sin_b).astype(BF16)

        for n in range(2):
            k = rope(acc[:, pl.ds(qw + n * 128, 128)])
            v = acc[:, pl.ds(qw + (n + 2) * 128, 128)].astype(BF16)
            abuf[:, pl.ds(qw + n * 128, 128)] = k
            abuf[:, pl.ds(qw + (n + 2) * 128, 128)] = v
            kc[l, n] = (k.astype(F32) * live).astype(BF16)
            vc[l, n] = (v.astype(F32) * live).astype(BF16)

        group = heads // 2

        def body(i):
            for n in range(2):
                lanes = pl.ds(pl.multiple_of((n * group + i) * 128, 128), 128)
                q = rope(acc[:, lanes])
                k = abuf[:, pl.ds(qw + n * 128, 128)]
                v = abuf[:, pl.ds(qw + (n + 2) * 128, 128)]
                s = lax.dot_general(q, k, (((1,), (1,)), ((), ())), preferred_element_type=F32) * scale
                s = jnp.where(mask[...] > 0.5, s, -1e30)
                e = jnp.exp(s - jnp.max(s, axis=-1, keepdims=True))
                p = (e / jnp.sum(e, axis=-1, keepdims=True)).astype(BF16)
                abuf[:, lanes] = jnp.dot(p, v, preferred_element_type=F32).astype(BF16)

        loop(group, body)

    def rs_drain():
        def body(j):
            d_copy(j).wait_send()
            x_copy(j).wait_send()
        loop(nch, body)

    def project_out(l):
        def group(i):
            slot = nq + i
            weights_ready(slot)

            def chunk(n):
                j = i * kper + n
                w = wbuf[slot, pl.ds(pl.multiple_of(n * qw, qw), qw), :]
                pbuf[:, cols(j)] = jnp.dot(abuf[:, pl.ds(0, qw)], w, preferred_element_type=F32).astype(BF16)
                d_copy(j).start()

                @pl.when(j >= 1)
                def _():
                    rs_mid(j - 1)

            loop(kper, chunk)
            fetch_u(l, nq + i, slot)

        loop(nq, group)
        rs_mid(nch - 1)
        loop(nch, lambda j: (rs_fin(j), None)[1])
        rs_drain()

    def mlp_up(l):
        clear(d)
        forward(0)

        def group(i):
            slot = i % RING

            @pl.when(i + 1 < nch)
            def _():
                forward(i + 1)
            gathered(i)
            weights_ready(slot)
            hk = hbuf[:, cols(i)]
            for n in range(nch):
                acc[:, pl.ds(n * CH, CH)] += jnp.dot(
                    hk, wbuf[slot, pl.ds(n * CH, CH), :], preferred_element_type=F32)

            @pl.when(i < nch - RING)
            def _():
                fetch_u(l, i + RING, slot)

            @pl.when(i >= nch - RING)
            def _():
                fetch_d(l, i + RING - nch, slot)

        loop(nch, group)
        gather_sent()

        def square(j):
            u = jnp.maximum(acc[:, cols(j)], 0.0)
            abuf[:, cols(j)] = (u * u).astype(BF16)

        loop(nch, square)

    def finish(j):
        hbuf[own_rows, cols(j)] = rs_fin(j)
        gx_copy(j).start()
        gc_copy(j).start()

    def mlp_down(l):
        last = l + 1 == layers

        def group(j):
            slot = j % RING
            weights_ready(slot)
            pbuf[:, cols(j)] = jnp.dot(abuf[...], wbuf[slot], preferred_element_type=F32).astype(BF16)
            d_copy(j).start()

            @pl.when(j < nch - RING)
            def _():
                fetch_d(l, j + RING, slot)
            if not last:
                @pl.when((j >= nch - RING) & (j < nch - RING + nq))
                def _():
                    fetch_q(l + 1, j - (nch - RING), slot)

                @pl.when(j >= nch - RING + nq)
                def _():
                    fetch_o(l + 1, j - (nch - RING + nq), slot)

            @pl.when(j >= 1)
            def _():
                rs_mid(j - 1)
            if last:
                @pl.when(j >= 3)
                def _():
                    finish(j - 3)

                @pl.when(j >= 5)
                def _():
                    forward(j - 5)

        loop(nch, group)
        rs_mid(nch - 1)
        if not last:
            loop(nch, lambda j: (rs_fin(j), None)[1])
        else:
            for j in range(nch - 3, nch):
                finish(j)
            for j in range(nch - 5, nch):
                forward(j)
            loop(nch, gathered)
        rs_drain()

    load = pltpu.make_async_copy(hid.at[0], pbuf, iosem.at[0])
    load.start()
    for kk in range(KV_RING):
        kv_fetch(0, kk)
    for i in range(nq):
        fetch_q(0, i, i)
    for i in range(nq):
        fetch_o(0, i, nq + i)

    barrier = pltpu.get_barrier_semaphore()
    for peer in (core_peer, chip_peer):
        pl.semaphore_signal(barrier, inc=1, device_id=peer, device_id_type=MESH)
    pl.semaphore_wait(barrier, 2)

    load.wait()
    xres[...] = pbuf[own_rows, :]

    def first_norm(b):
        rows = pl.ds(pl.multiple_of(b * quarter, quarter), quarter)
        norm_rows(pbuf, rows, rows, 0, lambda j: None)

    loop(4, first_norm)

    for l in range(layers):
        project(l)
        attention(l)
        project_out(l)
        norm_and_send(2 * l + 1)
        mlp_up(l)
        mlp_down(l)
        if l + 1 < layers:
            norm_and_send(2 * l + 2)

    gather_sent()
    store = pltpu.make_async_copy(hbuf, out.at[0], iosem.at[1])
    store.start()
    store.wait()


def solution(mesh):
    def device_body(hidden_in, lengths, positions, ln_gain, ln_bias, w_query, w_key, w_value, w_out, w_up, w_down):
        seq, d = hidden_in.shape[1], hidden_in.shape[2]
        layers, _, heads, head = w_query.shape
        kv_heads = w_key.shape[2]
        tp = mesh.shape["tp"]
        kv = kv_heads // tp
        nch = d // CH

        half_rot = head // 4
        lane = jnp.arange(head)
        freq = ROPE_BASE ** (-2.0 * jnp.arange(half_rot, dtype=F32) / (2 * half_rot))
        angle = positions[0].astype(F32)[:, None] * freq
        cos, sin = jnp.cos(angle), jnp.sin(angle)
        zero, one = jnp.zeros((seq, half_rot), F32), jnp.ones((seq, 2 * half_rot), F32)
        zero2 = jnp.zeros((seq, 2 * half_rot), F32)
        tabs = jnp.stack([
            jnp.concatenate([cos, cos, one], -1),
            jnp.concatenate([-sin, zero, zero2], -1),
            jnp.concatenate([zero, sin, zero2], -1)])
        pos = jnp.arange(seq)
        mask = ((pos[None, :] <= pos[:, None]) & (pos[None, :] < lengths[0])).astype(F32)
        valid = jnp.broadcast_to((pos < lengths[0]).astype(F32)[:, None], (seq, head))

        vmem = pl.BlockSpec(memory_space=pltpu.VMEM)
        anym = pl.BlockSpec(memory_space=pl.ANY)
        dma = pltpu.SemaphoreType.DMA
        cfg = (layers, seq, d, heads, head ** -0.5)
        out, kc, vc = pl.pallas_call(
            functools.partial(kernel, cfg),
            out_shape=(jax.ShapeDtypeStruct((1, seq, d), BF16),
                       jax.ShapeDtypeStruct((layers, kv, seq, head), BF16),
                       jax.ShapeDtypeStruct((layers, kv, seq, head), BF16)),
            in_specs=[anym, vmem, vmem, vmem, vmem, vmem] + [anym] * 6,
            out_specs=(anym, vmem, vmem),
            scratch_shapes=[
                pltpu.VMEM((RING, d, CH), BF16),
                pltpu.VMEM((KV_RING, CH, kv, head), BF16),
                pltpu.VMEM((KV_RING, CH, kv, head), BF16),
                pltpu.VMEM((CH, CH), BF16),
                pltpu.VMEM((seq, d), BF16),
                pltpu.VMEM((seq, d), F32),
                pltpu.VMEM((seq, d), BF16),
                pltpu.VMEM((seq, d), BF16),
                pltpu.VMEM((seq // 2, d), BF16),
                pltpu.VMEM((seq // 4, d), BF16),
                pltpu.VMEM((seq // 4, d), BF16),
                dma((RING,)), dma((KV_RING,)), dma((KV_RING,)), dma((2,)),
            ] + [dma((nch,))] * 10,
            compiler_params=pltpu.CompilerParams(
                collective_id=0, has_side_effects=True, vmem_limit_bytes=67043328),
            name="decoder_layers",
        )(hidden_in, tabs, mask, valid,
          ln_gain.reshape(2 * layers, d), ln_bias.reshape(2 * layers, d),
          w_query.transpose(0, 2, 1, 3),
          w_key.reshape(layers, d, tp, kv, head), w_value.reshape(layers, d, tp, kv, head),
          w_out.reshape(layers, heads * head, d), w_up, w_down)
        kc = kc.transpose(0, 2, 1, 3)[:, None]
        vc = vc.transpose(0, 2, 1, 3)[:, None]
        return out, kc, vc

    specs_in = (P("dp", None, None), P("dp"), P("dp", None), P(), P(), P(None, None, "tp", None), P(), P(),
                P(None, "tp", None, None), P(None, None, "tp"), P(None, "tp", None))
    cache_spec = P(None, "dp", None, "tp", None)
    return jax.shard_map(device_body, mesh=mesh, in_specs=specs_in,
                         out_specs=(P("dp", None, None), cache_spec, cache_spec), check_vma=False)
```

time: 613 us -> 273 us (0.45); the launches traced: 603 us -> 273 us
  Pallas kernels: 0 us -> 257 us
  waiting for transfers between devices: 221 us -> 0 us
  matrix products: 178 us -> 0 us
  local copies, waits for them, and re-layouts: 163 us -> 11.9 us
  other arithmetic: 25.3 us -> 2.91 us
  between operations: 15.7 us -> 1.32 us
    pallas_call x0 -> x1, Pallas kernels: none -> 257 us  [device_body(): pl.pallas_call(functools.partial(kernel, cfg), out_shape=(jax.ShapeDtypeS...]
    psum x4 -> x0, waiting for transfers between devices: 221 us -> none  [the longest x2 132 us: device_body(): attn_sum = lax.psum(attn_part, 'tp')]
    dot_general x12 -> x0, matrix products: 154 us -> none  [the longest x2 62.9 us: device_body(): jnp.einsum('bsd,df->bsf', normed_mlp, w_up[layer], preferred_element_type...]
    slice x6 -> x0, local copies, waits for them, and re-layouts: 56.5 us -> none  [the longest x1 24.7 us: device_body(): w_query[layer]]
    unnamed x102 -> x3, local copies, waits for them, and re-layouts: 54 us -> 7.73 us
    dynamic_slice x5 -> x0, local copies, waits for them, and re-layouts: 40.5 us -> none  [the longest x3 28 us: device_body(): lax.dynamic_slice_in_dim(w_key[layer], kv_start, kv_local, axis=1)]
    unnamed x4 -> x0, matrix products: 23.9 us -> none
    reduce_sum x10 -> x0, other arithmetic: 16.1 us -> none  [the longest x4 10.9 us: layer_norm(): average = jnp.mean(values, axis=-1, keepdims=True)]
  transfers between devices with their start and end apart: 4 -> 0, of which waited for: 4 -> 0; matrix products, arithmetic and copies ran while one was open for 7% -> 0% of each run, Pallas kernels for 0% -> 0%
where the time goes in v1:
time: 273 us
  Pallas kernels  257 us (94%)
  local copies, waits for them, and re-layouts  11.9 us (4%)
  other arithmetic  2.91 us (1%)
    pallas_call x1, Pallas kernels, device_body(): pl.pallas_call(functools.partial(kernel, cfg), out_shape=(jax.ShapeDtypeS...  257 us
    unnamed x3, local copies, waits for them, and re-layouts  7.73 us

profile of v1, /device:TPU:0, one launch (start us, length us, event | category | flops | bytes accessed | tf_op | source)
XLA Modules:
  0.0 273.1 jit_solution(13345571196399900295)
XLA Ops:
  1.3 0.1 pad.11.clone
  1.4 0.1 pad.8.clone
  1.5 0.7 convert_element_type.20
  2.1 1.6 reshape.42.gain
  3.7 1.6 reshape.43.bias
  5.4 0.8 broadcast_in_dim.29.valid
  6.1 0.7 fusion.1.mask
  6.8 0.5 multiply_cosine_fusion
  7.4 0.2 maximum_bitcast_fusion.1
  7.6 0.8 pad_maximum_fusion.tabs
  8.3 257.0 %decoder_layers.1 = (bf16[1,256,6144]{2,1,0:T(8,128)(2,1)}, bf16[2,2,256,128]{3,2,1,0:T(8,128)(2,1)}, bf16[2,2,256,128]{3,2,1,0:T(8,128)(2,1)}) custom-call(bf16[1,256,6144]{2,1,0:T(8,128)(2,1)} %hid.1, f32[3,256,128]{2,1,0:T(8,128)} %pad_maximum_fusion.tabs, f32[256,256]{1,0:T(8,128)} %fusion.1.mask, f32[256,128]{1,0:T(8,128)} %broadcast_in_dim.29.valid, ...), custom_call_target="tpu_custom_call" | custom-call | tf_op jit(solution)/shard_map/decoder_layers/pallas_call | solution.py:432
  265.4 1.9 copy.14
  267.3 1.9 copy.15
  269.2 3.9 %copy.18 = bf16[1,256,6144]{2,1,0:T(8,128)(2,1)} copy(bf16[1,256,6144]{2,1,0:T(8,128)(2,1)} %get-tuple-element.23) | data formatting | bytes 6291456
  (5 shorter events, 0.0 us)

commit v2 on v1

v2 whole, which is shorter than its diff:
```python
import functools

import jax
import jax.numpy as jnp
from jax import lax
from jax.experimental import pallas as pl
from jax.experimental.pallas import tpu as pltpu
from jax.sharding import PartitionSpec as P

ROPE_BASE = 10000.0
NORM_EPS = 1e-5
CH = 512
RING = 6
KV_RING = 2
LAG = 2
EARLY = 2
VMEM_LIMIT = 63360000
MESH = pl.DeviceIdType.MESH
F32 = jnp.float32
BF16 = jnp.bfloat16


def kernel(cfg, lens, hid, tabs, gain, bias, wq, wk, wv, wo, wu, wd,
           hbuf, kc, vc,
           wbuf, kraw, vraw, wkv, kvs, acc, abuf, pbuf, rbuf, xrecv, xres,
           wsem, ksem, vsem, iosem,
           d_send, d_recv, x_send, x_recv,
           gx_send, gx_recv, gc_send, gc_recv, gf_send, gf_recv):
    layers, seq, d, heads, scale = cfg
    nch = d // CH
    qw = heads * 128
    nq = qw // CH
    half = seq // 2
    part = half // 4
    kper = nch // nq
    both = slice(None)
    spare = heads + 4

    me = lax.axis_index("tp")
    mx = me // 2
    mc = me % 2
    core_peer = {"tp": mx * 2 + (1 - mc)}
    chip_peer = {"tp": (1 - mx) * 2 + mc}
    own = 2 * mc + mx
    peer = 2 * mc + 1 - mx
    away = pl.ds(2 * (1 - mc), 2)
    length = lens[0]

    def cols(j):
        if isinstance(j, int):
            return pl.ds(j * CH, CH)
        return pl.ds(pl.multiple_of(j * CH, CH), CH)

    def loop(n, body):
        lax.fori_loop(0, n, lambda i, c: (body(i), c)[1], 0)

    def sem(hf, j):
        return j if hf is both else hf * nch + j

    def span(hf, j):
        width = CH if hf is both else 2 * CH
        return pl.ds(j * width if isinstance(j, int) else pl.multiple_of(j * width, width), width)

    def spans(hf):
        return nch if hf is both else nch // 2

    def fetch_q(l, i, slot):
        rows = kper * CH
        for n in range(nq):
            for hh in range(4):
                pltpu.make_async_copy(
                    wq.at[l, 4 * n + hh, pl.ds(pl.multiple_of(i * rows, rows), rows), :],
                    wbuf.at[slot, pl.ds(n * rows, rows), pl.ds(hh * 128, 128)],
                    wsem.at[slot]).start()

    def fetch_o(l, i, slot):
        for n in range(kper):
            pltpu.make_async_copy(
                wo.at[l, :, cols(i * kper + n)],
                wbuf.at[slot, pl.ds(n * qw, qw), :],
                wsem.at[slot]).start()

    def fetch_u(l, i, slot):
        for n in range(nch):
            pltpu.make_async_copy(
                wu.at[l, cols(i), pl.ds(n * CH, CH)],
                wbuf.at[slot, pl.ds(n * CH, CH), :],
                wsem.at[slot]).start()

    def fetch_d(l, i, slot):
        pltpu.make_async_copy(wd.at[l, :, cols(i)], wbuf.at[slot], wsem.at[slot]).start()

    def weights_ready(slot):
        pltpu.make_async_copy(wd.at[0, :, pl.ds(0, CH)], wbuf.at[slot], wsem.at[slot]).wait()

    def kv_copies(l, kk):
        slot = kk % KV_RING
        rows = cols(kk)
        return (pltpu.make_async_copy(wk.at[l, rows, me], kraw.at[slot], ksem.at[slot]),
                pltpu.make_async_copy(wv.at[l, rows, me], vraw.at[slot], vsem.at[slot]))

    def kv_fetch(l, kk):
        for c in kv_copies(l, kk):
            c.start()

    def unpack(l, kk):
        for c in kv_copies(l, kk):
            c.wait()
        ks = kk % KV_RING

        size = 2 * part

        def piece(b):
            rows = pl.ds(pl.multiple_of(b * size, size), size)
            out = pl.ds(pl.multiple_of(kk * CH + b * size, size), size)
            for m, raw in enumerate((kraw, vraw)):
                acc[spare + m, pl.ds(0, 2 * size), :] = raw[ks, rows].astype(F32).reshape(2 * size, 128)
            for m in range(2):
                for n in range(2):
                    wkv[out, pl.ds((2 * m + n) * 128, 128)] = (
                        acc[spare + m, pl.ds(n, size, stride=2), :].astype(BF16))

        loop(CH // size, piece)

        @pl.when(kk + KV_RING < nch)
        def _():
            kv_fetch(l, kk + KV_RING)
        if l + 1 < layers:
            @pl.when(kk + KV_RING >= nch)
            def _():
                kv_fetch(l + 1, kk + KV_RING - nch)

    def remote(src, dst, ssem, rsem, peer_id):
        return pltpu.make_async_remote_copy(
            src_ref=src, dst_ref=dst, send_sem=ssem, recv_sem=rsem,
            device_id=peer_id, device_id_type=MESH)

    def d_copy(hf, j):
        i = sem(hf, j)
        return remote(pbuf.at[hf, away, :, span(hf, j)], rbuf.at[hf, :, :, span(hf, j)],
                      d_send.at[i], d_recv.at[i], core_peer)

    def x_copy(hf, j):
        i = sem(hf, j)
        return remote(pbuf.at[hf, peer, :, span(hf, j)], xrecv.at[hf, :, span(hf, j)],
                      x_send.at[i], x_recv.at[i], chip_peer)

    def rs_mid(hf, j):
        d_copy(hf, j).wait_recv()
        s = pbuf[hf, peer, :, span(hf, j)].astype(F32) + rbuf[hf, 1 - mx, :, span(hf, j)].astype(F32)
        pbuf[hf, peer, :, span(hf, j)] = s.astype(BF16)
        x_copy(hf, j).start()

    def rs_fin(hf, j):
        x_copy(hf, j).wait_recv()
        s = pbuf[hf, own, :, span(hf, j)].astype(F32) + rbuf[hf, mx, :, span(hf, j)].astype(F32)
        s = (s + xrecv[hf, :, span(hf, j)].astype(F32)).astype(BF16)
        new = (xres[hf, :, span(hf, j)].astype(F32) + s.astype(F32)).astype(BF16)
        xres[hf, :, span(hf, j)] = new
        return new

    def rs_fin_all(hf):
        loop(spans(hf), lambda j: (rs_fin(hf, j), None)[1])

    def rs_drain(hf):
        def body(j):
            d_copy(hf, j).wait_send()
            x_copy(hf, j).wait_send()
        loop(spans(hf), body)

    def gx_copy(hf, j):
        r, i = hbuf.at[hf, own, :, span(hf, j)], sem(hf, j)
        return remote(r, r, gx_send.at[i], gx_recv.at[i], chip_peer)

    def gc_copy(hf, j):
        r, i = hbuf.at[hf, own, :, span(hf, j)], sem(hf, j)
        return remote(r, r, gc_send.at[i], gc_recv.at[i], core_peer)

    def gf_copy(hf, j):
        r, i = hbuf.at[hf, peer, :, span(hf, j)], sem(hf, j)
        return remote(r, r, gf_send.at[i], gf_recv.at[i], core_peer)

    def gather_send(hf, j):
        gx_copy(hf, j).start()
        gc_copy(hf, j).start()

    def forward(hf, j):
        gx_copy(hf, j).wait_recv()
        gf_copy(hf, j).start()

    def gathered(hf, j):
        gc_copy(hf, j).wait_recv()
        gf_copy(hf, j).wait_recv()

    def gather_sent(hf):
        def body(j):
            gx_copy(hf, j).wait_send()
            gc_copy(hf, j).wait_send()
            gf_copy(hf, j).wait_send()
        loop(spans(hf), body)

    def norm(rows, load, layer, which, store):
        def fold(x):
            return sum(x[:, k * 128:(k + 1) * 128] for k in range(CH // 128))

        zero = jnp.zeros((rows, 128), F32)
        total = lax.fori_loop(0, nch, lambda j, t: t + fold(load(j)), zero)
        mean = jnp.sum(total, axis=-1, keepdims=True) * (1.0 / d)

        def squares(j, t):
            x = load(j) - mean
            return t + fold(x * x)

        var = jnp.sum(lax.fori_loop(0, nch, squares, zero), axis=-1, keepdims=True) * (1.0 / d)
        rstd = lax.rsqrt(var + NORM_EPS)

        def write(j):
            x = (load(j) - mean) * rstd
            g = gain[layer, pl.ds(which, 1), cols(j)]
            b = bias[layer, pl.ds(which, 1), cols(j)]
            store(j, (x * (1.0 + g) + b).astype(BF16))

        loop(nch, write)

    def norm_own(hf, layer, which, sent):
        def store(j, y):
            hbuf[hf, own, :, cols(j)] = y

            @pl.when((j % 2 == 1) & (j < 2 * sent))
            def _():
                gather_send(hf, j // 2)

        norm(part, lambda j: xres[hf, :, cols(j)].astype(F32), layer, which, store)

    def clear(first, count, blocks):
        def body(i):
            acc[i, pl.ds(first, count), :] = jnp.zeros((count, 128), F32)
        loop(blocks, body)

    def add(n, first, count, value):
        for t in range(CH // 128):
            acc[n * (CH // 128) + t, pl.ds(first, count), :] += value[:, t * 128:(t + 1) * 128]

    def project(l, hf):
        rows, count = (0, seq) if hf is both else (hf * half, half)
        clear(rows, count, spare)
        if l > 0:
            forward(hf, 0)

        def group(i):
            if hf is both or hf == 0:
                weights_ready(i)

            def chunk(kq):
                kk = i * kper + kq
                if l > 0:
                    if hf == 0:
                        unpack(l, kk)

                    @pl.when((kk % 2 == 0) & (kk + 2 < nch))
                    def _():
                        forward(hf, kk // 2 + 1)

                    @pl.when(kk % 2 == 0)
                    def _():
                        gathered(hf, kk // 2)
                hk = hbuf[hf, :, :, cols(kk)].reshape(count, CH)
                for n in range(nq):
                    w = wbuf[i, pl.ds(pl.multiple_of(n * kper * CH + kq * CH, CH), CH), :]
                    add(n, rows, count, jnp.dot(hk, w, preferred_element_type=F32))
                add(nq, rows, count, jnp.dot(hk, wkv[cols(kk), :], preferred_element_type=F32))

            loop(kper, chunk)
            if hf is both or hf == 1:
                fetch_u(l, i, i)

        loop(nq, group)

    def attention(l, hf):
        cosine, sin_a, sin_b = (tabs[t, pl.ds(hf * half, half), :] for t in range(3))
        rows, width = pl.ds(hf * half, half), seq
        row = lax.broadcasted_iota(jnp.int32, (half, 128), 0) + hf * half
        live = row < length

        def rope(x):
            return x * cosine + pltpu.roll(x, 96, 1) * sin_a + pltpu.roll(x, 32, 1) * sin_b

        for n in range(2):
            k = rope(acc[heads + n, rows, :])
            v = acc[heads + 2 + n, rows, :]
            kvs[rows, pl.ds(n * 128, 128)] = k.astype(BF16)
            kvs[rows, pl.ds((n + 2) * 128, 128)] = v.astype(BF16)
            acc[spare, pl.ds(n, half, stride=2), :] = jnp.where(live, k, 0.0)
            acc[spare + 1, pl.ds(n, half, stride=2), :] = jnp.where(live, v, 0.0)
        kc[l, 0, rows] = acc[spare].reshape(half, 2, 128).astype(BF16)
        vc[l, 0, rows] = acc[spare + 1].reshape(half, 2, 128).astype(BF16)

        group = heads // 2
        limit = jnp.minimum(lax.broadcasted_iota(jnp.int32, (half, width), 0) + hf * half, length - 1)
        allowed = lax.broadcasted_iota(jnp.int32, (half, width), 1) <= limit
        pace = scale * 1.4426950408889634

        def body(i):
            for n in range(2):
                k = kvs[:, pl.ds(n * 128, 128)]
                v = kvs[:, pl.ds((n + 2) * 128, 128)]
                for t in range(2):
                    j = n * group + 2 * i + t
                    lanes = pl.ds(pl.multiple_of(j * 128, 128), 128)
                    q = rope(acc[j, rows, :]).astype(BF16)
                    s = lax.dot_general(q, k, (((1,), (1,)), ((), ())), preferred_element_type=F32)
                    s = jnp.where(allowed, s, -1e30)
                    e = jnp.exp2((s - jnp.max(s, axis=-1, keepdims=True)) * pace)
                    p = (e * (1.0 / jnp.sum(e, axis=-1, keepdims=True))).astype(BF16)
                    abuf[rows, lanes] = jnp.dot(p, v, preferred_element_type=F32).astype(BF16)

        loop(group // 2, body)

    def project_out(l, hf):
        rows = pl.ds(hf * half, half)

        def group(i):
            slot = nq + i
            if hf == 0:
                weights_ready(slot)

            def pair(n):
                j = i * (kper // 2) + n
                for t in range(2):
                    w = wbuf[slot, pl.ds(pl.multiple_of((2 * n + t) * qw, qw), qw), :]
                    o = jnp.dot(abuf[rows, pl.ds(0, qw)], w, preferred_element_type=F32)
                    pbuf[hf, :, :, cols(2 * j + t)] = o.astype(BF16).reshape(4, part, CH)
                d_copy(hf, j).start()

                @pl.when(j >= LAG)
                def _():
                    rs_mid(hf, j - LAG)

            loop(kper // 2, pair)
            if hf == 1:
                fetch_u(l, slot, slot)

        loop(nq, group)

    def mlp_up(l):
        clear(0, seq, d // 128)
        forward(0, 0)
        forward(1, 0)

        def group(i):
            slot = i % RING

            @pl.when((i % 2 == 0) & (i + 2 < nch))
            def _():
                forward(0, i // 2 + 1)
                forward(1, i // 2 + 1)

            @pl.when(i % 2 == 0)
            def _():
                gathered(0, i // 2)
                gathered(1, i // 2)
            weights_ready(slot)
            hk = hbuf[:, :, :, cols(i)].reshape(seq, CH)
            for n in range(nch):
                add(n, 0, seq, jnp.dot(hk, wbuf[slot, pl.ds(n * CH, CH), :], preferred_element_type=F32))

            @pl.when(i < nch - RING)
            def _():
                fetch_u(l, i + RING, slot)

            @pl.when(i >= nch - RING)
            def _():
                fetch_d(l, i + RING - nch, slot)

        loop(nch, group)
        gather_sent(0)
        gather_sent(1)

        def square(j):
            for t in range(4):
                u = jnp.maximum(acc[4 * j + t], 0.0)
                abuf[:, pl.ds(pl.multiple_of(j * CH + t * 128, 128), 128)] = (u * u).astype(BF16)

        loop(nch, square)

    def finish(j):
        hbuf[:, own, :, cols(j)] = rs_fin(both, j)
        gather_send(both, j)

    def mlp_down(l):
        last = l + 1 == layers

        def group(j):
            slot = j % RING
            weights_ready(slot)
            m = jnp.dot(abuf[...], wbuf[slot], preferred_element_type=F32)
            pbuf[:, :, :, cols(j)] = m.astype(BF16).reshape(2, 4, part, CH)
            d_copy(both, j).start()

            @pl.when(j < nch - RING)
            def _():
                fetch_d(l, j + RING, slot)
            if not last:
                @pl.when((j >= nch - RING) & (j < nch - RING + nq))
                def _():
                    fetch_q(l + 1, j - (nch - RING), slot)

                @pl.when(j >= nch - RING + nq)
                def _():
                    fetch_o(l + 1, j - (nch - RING + nq), slot)

            @pl.when(j >= 1)
            def _():
                rs_mid(both, j - 1)
            if last:
                @pl.when(j >= 3)
                def _():
                    finish(j - 3)

                @pl.when(j >= 5)
                def _():
                    forward(both, j - 5)

        loop(nch, group)
        rs_mid(both, nch - 1)
        if not last:
            rs_fin_all(both)
        else:
            for j in range(nch - 3, nch):
                finish(j)
            for j in range(nch - 5, nch):
                forward(both, j)
            loop(nch, lambda j: gathered(both, j))
        rs_drain(both)

    load = pltpu.make_async_copy(hid, pbuf, iosem.at[0])
    load.start()
    for kk in range(KV_RING):
        kv_fetch(0, kk)
    barrier = pltpu.get_barrier_semaphore()
    for other in (core_peer, chip_peer):
        pl.semaphore_signal(barrier, inc=1, device_id=other, device_id_type=MESH)
    load.wait()

    for i in range(nq):
        fetch_q(0, i, i)
    xres[...] = pbuf[:, own]
    kvs[pl.ds(half, half), :] = jnp.zeros((half, CH), BF16)

    def first_norm(b):
        hf, o = b // 2, pl.ds(b % 2 * 2, 2)

        def store(j, y):
            hbuf[hf, o, :, cols(j)] = y.reshape(2, part, CH)

        norm(2 * part, lambda j: pbuf[hf, o, :, cols(j)].reshape(2 * part, CH).astype(F32), 0, 0, store)

    loop(4, first_norm)
    loop(nch, lambda kk: unpack(0, kk))
    for i in range(nq):
        fetch_o(0, i, nq + i)
    pl.semaphore_wait(barrier, 2)

    for l in range(layers):
        project(l, 0 if l > 0 else both)
        if l > 0:
            gather_sent(0)
        attention(l, 0)
        project_out(l, 0)
        loop(LAG, lambda j: rs_mid(0, spans(0) - LAG + j))
        if l > 0:
            project(l, 1)
            gather_sent(1)
        attention(l, 1)
        project_out(l, 1)
        loop(LAG, lambda j: rs_mid(1, spans(1) - LAG + j))
        rs_fin_all(0)
        norm_own(0, l, 1, EARLY)
        rs_fin_all(1)
        norm_own(1, l, 1, EARLY)

        def rest(j):
            gather_send(0, EARLY + j)
            gather_send(1, EARLY + j)

        loop(spans(0) - EARLY, rest)
        rs_drain(0)
        rs_drain(1)
        mlp_up(l)
        mlp_down(l)
        if l + 1 < layers:
            norm_own(0, l + 1, 0, spans(0))
            norm_own(1, l + 1, 0, spans(1))

    gather_sent(both)


def solution(mesh):
    def device_body(hidden_in, lengths, positions, ln_gain, ln_bias, w_query, w_key, w_value, w_out, w_up, w_down):
        seq, d = hidden_in.shape[1], hidden_in.shape[2]
        layers, _, heads, head = w_query.shape
        kv_heads = w_key.shape[2]
        tp = mesh.shape["tp"]
        kv = kv_heads // tp
        nch = d // CH

        half_rot = head // 4
        lane = jnp.arange(head)
        freq = ROPE_BASE ** (-2.0 * (lane % half_rot).astype(F32) / (2 * half_rot))
        angle = positions[0].astype(F32)[:, None] * freq
        cos, sin = jnp.cos(angle), jnp.sin(angle)
        tabs = jnp.stack([
            jnp.where(lane < 2 * half_rot, cos, 1.0),
            jnp.where(lane < half_rot, -sin, 0.0),
            jnp.where((lane >= half_rot) & (lane < 2 * half_rot), sin, 0.0)])

        vmem = pl.BlockSpec(memory_space=pltpu.VMEM)
        smem = pl.BlockSpec(memory_space=pltpu.SMEM)
        anym = pl.BlockSpec(memory_space=pl.ANY)
        dma = pltpu.SemaphoreType.DMA
        cfg = (layers, seq, d, heads, head ** -0.5)
        rows = (2, 4, seq // 8)
        out, kc, vc = pl.pallas_call(
            functools.partial(kernel, cfg),
            out_shape=(pltpu.VMEM(rows + (d,), BF16),
                       pltpu.VMEM((layers, 1, seq, kv, head), BF16),
                       pltpu.VMEM((layers, 1, seq, kv, head), BF16)),
            in_specs=[smem, anym, vmem, vmem, vmem] + [anym] * 6,
            out_specs=(vmem, vmem, vmem),
            scratch_shapes=[
                pltpu.VMEM((RING, d, CH), BF16),
                pltpu.VMEM((KV_RING, CH, kv, head), BF16),
                pltpu.VMEM((KV_RING, CH, kv, head), BF16),
                pltpu.VMEM((d, 2 * kv * head), BF16),
                pltpu.VMEM((seq, 2 * kv * head), BF16),
                pltpu.VMEM((d // head, seq, head), F32),
                pltpu.VMEM((seq, d), BF16),
                pltpu.VMEM(rows + (d,), BF16),
                pltpu.VMEM((2, 2, seq // 8, d), BF16),
                pltpu.VMEM((2, seq // 8, d), BF16),
                pltpu.VMEM((2, seq // 8, d), BF16),
                dma((RING,)), dma((KV_RING,)), dma((KV_RING,)), dma((2,)),
            ] + [dma((2 * nch,))] * 10,
            compiler_params=pltpu.CompilerParams(
                collective_id=0, has_side_effects=True, vmem_limit_bytes=VMEM_LIMIT),
            name="decoder_layers",
        )(lengths, hidden_in.reshape(rows + (d,)), tabs, ln_gain, ln_bias,
          w_query.transpose(0, 2, 1, 3),
          w_key.reshape(layers, d, tp, kv, head), w_value.reshape(layers, d, tp, kv, head),
          w_out.reshape(layers, heads * head, d), w_up, w_down)
        return out.reshape(1, seq, d), kc, vc

    specs_in = (P("dp", None, None), P("dp"), P("dp", None), P(), P(), P(None, None, "tp", None), P(), P(),
                P(None, "tp", None, None), P(None, None, "tp"), P(None, "tp", None))
    cache_spec = P(None, "dp", None, "tp", None)
    return jax.shard_map(device_body, mesh=mesh, in_specs=specs_in,
                         out_specs=(P("dp", None, None), cache_spec, cache_spec), check_vma=False)
```

time: 273 us -> 234 us (0.86)
  Pallas kernels: 257 us -> 227 us
  local copies, waits for them, and re-layouts: 11.9 us -> 3.07 us
    pallas_call x1, Pallas kernels: 257 us -> 227 us  [device_body(): pl.pallas_call(functools.partial(kernel, cfg), out_shape=(pltpu.VMEM(rows...]
    unnamed x3, local copies, waits for them, and re-layouts: 7.73 us -> 3.07 us
    reshape x2 -> x0, local copies, waits for them, and re-layouts: 3.21 us -> none  [the longest x1 1.61 us: device_body(): ln_bias.reshape(2 * layers, d)]
where the time goes in v2:
time: 234 us
  Pallas kernels  227 us (97%)
  local copies, waits for them, and re-layouts  3.07 us (1%)
    pallas_call x1, Pallas kernels, device_body(): pl.pallas_call(functools.partial(kernel, cfg), out_shape=(pltpu.VMEM(rows...  227 us

profile of v2, /device:TPU:0, one launch (start us, length us, event | category | flops | bytes accessed | tf_op | source)
XLA Modules:
  0.0 233.7 jit_solution(2925635996459738792)
XLA Ops:
  1.3 0.7 convert_element_type.17
  2.0 0.5 fusion.3
  2.5 0.8 pad_maximum_fusion.tabs
  3.3 227.3 %decoder_layers.1 = (bf16[2,4,32,6144]{3,2,1,0:T(8,128)(2,1)S(1)}, bf16[2,1,256,2,128]{4,3,2,1,0:T(2,128)(2,1)S(1)}, bf16[2,1,256,2,128]{4,3,2,1,0:T(2,128)(2,1)S(1)}) custom-call(s32[1]{0:T(128)S(6)} %copy.20.lens, bf16[2,4,32,6144]{3,2,1,0:T(8,128)(2,1)} %bitcast.12, f32[3,256,128]{2,1,0:T(8,128)} %pad_maximum_fusion.tabs, f32[2,2,6144]{2,1,0:T(2,128)} %gain.1, ...), custom_call_target="tpu_custom_call" | custom-call | tf_op jit(solution)/shard_map/decoder_layers/pallas_call | solution.py:523
  230.6 1.7 copy.17
  232.3 0.7 copy.18
  233.0 0.7 copy.19
  (3 shorter events, 0.0 us)
